TPU v7x, 32 devices: a whole 2x2x4 slice. The times are simulated.
32 devices in a mesh: seq: 8 (over z, y), rep: 4 (over x, core).
Axes of the slice: x: 2, y: 2, z: 4, core: 2. Of those that a mesh axis runs over, the one named last changes fastest.
Arguments:
- head_out: bfloat16 [4, 4096, 4096], P('rep', 'seq'), may hold values from -6 to 6
- grad_out: bfloat16 [4, 4096, 3584], P('rep', 'seq'), may hold values from -6 to 6
- hash_codes: int32 [4, 16, 3584], P('rep'), may hold values from 0 to 511
- loss_mask: int32 [4096], P('seq'), may hold values 0 or 1
- query_ids: int32 [64], replicated, may hold values from 0 to 4095
Outputs:
- attribution: float32 [4096, 64], P(('seq', 'rep'))
All inputs are finite; a program needn't handle non-finite values. No bound on the sum of `loss_mask` on one device may be relied on, other than what follows from the above.
Results may differ from a plain program's by a relative error of at most 0.0025.
Values may be sent and summed in bfloat16 or wider, within the bound.
A program may use at most 64 MiB of HBM per device.

v0:
```python
import math

import jax
import jax.numpy as jnp
from jax import lax
from jax.sharding import PartitionSpec as P

ridge_shift = 0.25
norm_floor = 1e-06


def build_sketches(outputs, gradient, codes):
    head_count = codes.shape[0]
    sketch_width = outputs.shape[1] // head_count
    model_width = gradient.shape[1]
    sketch_scale = math.sqrt(sketch_width / model_width)
    columns = jnp.arange(sketch_width, dtype=jnp.int32)

    def one_head(head_index):
        head_codes = codes[head_index]
        bucket = head_codes % sketch_width
        sign_flip = 1 - 2 * (head_codes // sketch_width)
        count_table = jnp.where(bucket[:, None] == columns[None, :], sign_flip[:, None], 0).astype(
            jnp.bfloat16
        )
        counted = jnp.dot(gradient, count_table, preferred_element_type=jnp.float32)
        picked = lax.dynamic_slice_in_dim(
            outputs, head_index * sketch_width, sketch_width, 1
        ).astype(jnp.float32)
        return (picked * counted * sketch_scale).astype(jnp.bfloat16)

    return lax.map(one_head, jnp.arange(head_count, dtype=jnp.int32))


def solve_queries(gram_sum, chosen, token_count):
    sketch_width = gram_sum.shape[0]
    gram_sum = gram_sum / token_count + ridge_shift * jnp.eye(sketch_width, dtype=jnp.float32)
    factor = jnp.linalg.cholesky(gram_sum)
    return jax.scipy.linalg.cho_solve((factor, True), chosen.T).astype(jnp.bfloat16)


def on_device(head_out, grad_out, hash_codes, loss_mask, query_ids):
    sketches = build_sketches(head_out[0], grad_out[0], hash_codes[0])
    tok_rows = loss_mask.shape[0]
    out_rows = tok_rows // lax.axis_size("rep")
    mask_bf = loss_mask.astype(jnp.bfloat16)
    local_count = jnp.sum(loss_mask.astype(jnp.float32))
    token_count = lax.psum(local_count, "seq") + 1.0
    local_grams = jnp.einsum(
        "htk,htj->hkj",
        sketches * mask_bf[None, :, None],
        sketches,
        preferred_element_type=jnp.float32,
    )
    first_row = lax.axis_index("seq") * tok_rows
    query_hits = (
        query_ids[:, None] - first_row == jnp.arange(tok_rows, dtype=jnp.int32)[None, :]
    ).astype(jnp.bfloat16)
    local_chosen = jnp.einsum(
        "qt,htk->hqk", query_hits, sketches, preferred_element_type=jnp.float32
    )
    own_grams, own_chosen = (
        lax.psum_scatter(local_grams, "seq", scatter_dimension=0, tiled=True),
        lax.psum_scatter(local_chosen, "seq", scatter_dimension=0, tiled=True),
    )
    solved = jnp.stack(
        [
            solve_queries(own_grams[slot_index], own_chosen[slot_index], token_count)
            for slot_index in range(own_grams.shape[0])
        ]
    )
    solved_all = lax.all_gather(solved, "seq", axis=0, tiled=True)
    score_sum = jnp.einsum("htk,hkq->tq", sketches, solved_all, preferred_element_type=jnp.float32)
    contrib = lax.psum_scatter(score_sum, "rep", scatter_dimension=0, tiled=True)
    row_start = lax.axis_index("rep") * out_rows
    mask_rows = lax.dynamic_slice_in_dim(loss_mask, row_start, out_rows, 0).astype(jnp.float32)
    partial_value = jnp.sum(mask_rows[:, None] * contrib * contrib, 0)
    norm_sum = lax.psum(partial_value, ("seq", "rep")) / token_count
    return contrib / jnp.sqrt(norm_sum + norm_floor)


def solution(mesh):
    placed = (P("rep", "seq", None), P("rep", "seq", None), P("rep", None, None), P("seq"), P())
    return jax.shard_map(
        on_device, mesh=mesh, in_specs=placed, out_specs=P(("seq", "rep"), None), check_vma=False
    )
```

profile of v0, /device:TPU:0, one launch (start us, length us, event | category | flops | bytes accessed | tf_op | source)
XLA Modules:
  0.0 561.4 jit_solution(14292173351317738377)
XLA Ops:
  6.5 6.5 %copy.13 = bf16[1,512,4096]{1,2,0:T(8,128)(2,1)} copy(bf16[1,512,4096]{2,1,0:T(8,128)(2,1)} %param.10) | data formatting | bytes 8388608 | tf_op args[0]
  13.0 158.3 %while.17 = (s32[]{:T(128)}, bf16[16,512,256]{1,2,0:T(8,128)(2,1)}, s32[16]{0:T(128)S(1)}, bf16[512,4096]{0,1:T(8,128)(2,1)}, s32[16,3584]{1,0:T(8,128)}, /*inde...) while((s32[]{:T(128)}, bf16[16,512,256]{1,2,0:T(8,128)(2,1)}, ...), condition=%wide.region_1.2_spmd.clone, body=%wide.region_0.1_spmd.clone.sunk | while | flops 942876160 | bytes 4295377 | solution.py:32
  46.5 6.1 %fusion.76 = bf16[16,512,256]{1,2,0:T(8,128)(2,1)} fusion(bf16[16,512,256]{1,2,0:T(8,128)(2,1)} %get-tuple-element.293, s32[]{:T(128)} %get-tuple-element.292, bf16[512,3584]{1,0:T(8,128)(2,1)} %get-tuple-element.308, s32[3584]{0:T(1024)S(1)} %get-tuple-element.267, s32[3584]{0:T(1024)S(1)} %get-tuple-element.268, ...), kind=kOutput, calls=%fused_computation.16.clone.1 | convolution fusion | flops 942800896 | bytes 4223492 | tf_op jit(solution)/shard_map/while/body/eval_jaxpr/dot_general | solution.py:26
  56.4 6.1 %fusion.76 = bf16[16,512,256]{1,2,0:T(8,128)(2,1)} fusion(bf16[16,512,256]{1,2,0:T(8,128)(2,1)} %get-tuple-element.293, s32[]{:T(128)} %get-tuple-element.292, bf16[512,3584]{1,0:T(8,128)(2,1)} %get-tuple-element.308, s32[3584]{0:T(1024)S(1)} %get-tuple-element.267, s32[3584]{0:T(1024)S(1)} %get-tuple-element.268, ...), kind=kOutput, calls=%fused_computation.16.clone.1 | convolution fusion | flops 942800896 | bytes 4223492 | tf_op jit(solution)/shard_map/while/body/eval_jaxpr/dot_general | solution.py:26
  66.3 6.1 %fusion.76 = bf16[16,512,256]{1,2,0:T(8,128)(2,1)} fusion(bf16[16,512,256]{1,2,0:T(8,128)(2,1)} %get-tuple-element.293, s32[]{:T(128)} %get-tuple-element.292, bf16[512,3584]{1,0:T(8,128)(2,1)} %get-tuple-element.308, s32[3584]{0:T(1024)S(1)} %get-tuple-element.267, s32[3584]{0:T(1024)S(1)} %get-tuple-element.268, ...), kind=kOutput, calls=%fused_computation.16.clone.1 | convolution fusion | flops 942800896 | bytes 4223492 | tf_op jit(solution)/shard_map/while/body/eval_jaxpr/dot_general | solution.py:26
  86.1 6.1 %fusion.76 = bf16[16,512,256]{1,2,0:T(8,128)(2,1)} fusion(bf16[16,512,256]{1,2,0:T(8,128)(2,1)} %get-tuple-element.293, s32[]{:T(128)} %get-tuple-element.292, bf16[512,3584]{1,0:T(8,128)(2,1)} %get-tuple-element.308, s32[3584]{0:T(1024)S(1)} %get-tuple-element.267, s32[3584]{0:T(1024)S(1)} %get-tuple-element.268, ...), kind=kOutput, calls=%fused_computation.16.clone.1 | convolution fusion | flops 942800896 | bytes 4223492 | tf_op jit(solution)/shard_map/while/body/eval_jaxpr/dot_general | solution.py:26
  115.7 6.1 %fusion.76 = bf16[16,512,256]{1,2,0:T(8,128)(2,1)} fusion(bf16[16,512,256]{1,2,0:T(8,128)(2,1)} %get-tuple-element.293, s32[]{:T(128)} %get-tuple-element.292, bf16[512,3584]{1,0:T(8,128)(2,1)} %get-tuple-element.308, s32[3584]{0:T(1024)S(1)} %get-tuple-element.267, s32[3584]{0:T(1024)S(1)} %get-tuple-element.268, ...), kind=kOutput, calls=%fused_computation.16.clone.1 | convolution fusion | flops 942800896 | bytes 4223492 | tf_op jit(solution)/shard_map/while/body/eval_jaxpr/dot_general | solution.py:26
  125.6 6.1 %fusion.76 = bf16[16,512,256]{1,2,0:T(8,128)(2,1)} fusion(bf16[16,512,256]{1,2,0:T(8,128)(2,1)} %get-tuple-element.293, s32[]{:T(128)} %get-tuple-element.292, bf16[512,3584]{1,0:T(8,128)(2,1)} %get-tuple-element.308, s32[3584]{0:T(1024)S(1)} %get-tuple-element.267, s32[3584]{0:T(1024)S(1)} %get-tuple-element.268, ...), kind=kOutput, calls=%fused_computation.16.clone.1 | convolution fusion | flops 942800896 | bytes 4223492 | tf_op jit(solution)/shard_map/while/body/eval_jaxpr/dot_general | solution.py:26
  165.2 6.1 %fusion.76 = bf16[16,512,256]{1,2,0:T(8,128)(2,1)} fusion(bf16[16,512,256]{1,2,0:T(8,128)(2,1)} %get-tuple-element.293, s32[]{:T(128)} %get-tuple-element.292, bf16[512,3584]{1,0:T(8,128)(2,1)} %get-tuple-element.308, s32[3584]{0:T(1024)S(1)} %get-tuple-element.267, s32[3584]{0:T(1024)S(1)} %get-tuple-element.268, ...), kind=kOutput, calls=%fused_computation.16.clone.1 | convolution fusion | flops 942800896 | bytes 4223492 | tf_op jit(solution)/shard_map/while/body/eval_jaxpr/dot_general | solution.py:26
  176.0 6.7 %fusion.17 = f32[16,256,256]{1,2,0:T(8,128)} fusion(bf16[16,512,256]{1,2,0:T(8,128)(2,1)} %get-tuple-element.99, bf16[512]{0:T(512)(128)(2,1)S(1)} %convert_element_type.36), kind=kOutput, calls=%fused_computation.29 | convolution fusion | flops 1075838976 | bytes 8389632 | tf_op jit(solution)/shard_map/htk,htj->hkj/dot_general | solution.py:49
  183.4 24.0 %psum.14 = f32[]{:T(128)} all-reduce(f32[]{:T(128)} %convert_reduce_fusion), channel_id=1, replica_groups=mesh['seq'=8,'rep'=4] {'seq'}, use_global_device_ids=true, to_apply=%region_4.5 | all-reduce | flops 1 | bytes 8 | tf_op jit(solution)/shard_map/psum | solution.py:48
  208.0 34.9 %reduce-scatter.6.cloned.1.call-done = f32[2,64,256]{2,1,0:T(8,128)} async-done(((f32[16,64,256]{2,1,0:T(8,128)}), f32[2,64,256]{2,1,0:T(8,128)}) %reduce-scatter.6.cloned.1.call-update) | async-done | bytes 131088 | tf_op jit(solution)/shard_map/reduce_scatter | solution.py:64
  243.8 90.0 %reduce-scatter.4.cloned.1.call-done = f32[2,256,256]{1,2,0:T(8,128)} async-done(((f32[16,256,256]{1,2,0:T(8,128)}), f32[2,256,256]{1,2,0:T(8,128)}) %reduce-scatter.4.cloned.1.call-update) | async-done | bytes 524304 | tf_op jit(solution)/shard_map/reduce_scatter | solution.py:63
  335.3 11.7 %cholesky.130 = f32[128,128]{1,0:T(8,128)S(1)} custom-call(f32[128,128]{1,0:T(8,128)S(1)} %cholesky.194), custom_call_target="Cholesky" | custom-call | tf_op jit(solution)/shard_map/jit(cholesky)/cholesky | solution.py:38
  347.0 9.8 %custom-call.15 = f32[1,128,128]{1,2,0:T(8,128)S(1)} custom-call(f32[1,128,128]{2,1,0:T(8,128)S(1)} %get-tuple-element.171), custom_call_target="InvertDiagBlocksLowerTriangular" | custom-call | tf_op jit(solution)/shard_map/jit(cholesky)/cholesky | solution.py:38
  357.3 11.7 %cholesky.147 = f32[128,128]{1,0:T(8,128)S(1)} custom-call(f32[128,128]{1,0:T(8,128)S(1)} %convolution_subtract_fusion.1), custom_call_target="Cholesky" | custom-call | tf_op jit(solution)/shard_map/jit(cholesky)/cholesky | solution.py:38
  375.4 19.9 %custom-call.16 = f32[2,128,128]{1,2,0:T(8,128)S(1)} custom-call(f32[2,128,128]{2,1,0:T(8,128)S(1)} %get-tuple-element.128), custom_call_target="InvertDiagBlocksLowerTriangular" | custom-call | tf_op jit(solution)/shard_map/jit(_cho_solve)/triangular_solve | solution.py:39
  396.8 11.7 %cholesky.164 = f32[128,128]{1,0:T(8,128)S(1)} custom-call(f32[128,128]{1,0:T(8,128)S(1)} %cholesky.197), custom_call_target="Cholesky" | custom-call | tf_op jit(solution)/shard_map/jit(cholesky)/cholesky | solution.py:38
  408.6 9.8 %custom-call.17 = f32[1,128,128]{1,2,0:T(8,128)S(1)} custom-call(f32[1,128,128]{2,1,0:T(8,128)S(1)} %get-tuple-element.175), custom_call_target="InvertDiagBlocksLowerTriangular" | custom-call | tf_op jit(solution)/shard_map/jit(cholesky)/cholesky | solution.py:38
  418.9 11.7 %cholesky.181 = f32[128,128]{1,0:T(8,128)S(1)} custom-call(f32[128,128]{1,0:T(8,128)S(1)} %convolution_subtract_fusion), custom_call_target="Cholesky" | custom-call | tf_op jit(solution)/shard_map/jit(cholesky)/cholesky | solution.py:38
  437.4 19.9 %custom-call.18 = f32[2,128,128]{1,2,0:T(8,128)S(1)} custom-call(f32[2,128,128]{2,1,0:T(8,128)S(1)} %get-tuple-element.129), custom_call_target="InvertDiagBlocksLowerTriangular" | custom-call | tf_op jit(solution)/shard_map/jit(_cho_solve)/triangular_solve | solution.py:39
  458.8 31.4 %all_gather.3 = bf16[16,256,64]{1,2,0:T(8,128)(2,1)S(1)} all-gather(bf16[2,256,64]{1,2,0:T(8,128)(2,1)S(1)} %pad_maximum_fusion), channel_id=1, replica_groups=mesh['seq'=8,'rep'=4] {'seq'}, dimensions={0}, use_global_device_ids=true | all-gather | bytes 589824 | tf_op jit(solution)/shard_map/all_gather | solution.py:72
  494.0 19.3 %reduce-scatter.8.cloned.1.call-done = f32[128,64]{0,1:T(8,128)} async-done(((f32[512,64]{0,1:T(8,128)}), f32[128,64]{0,1:T(8,128)}) %reduce-scatter.8.cloned.1.call-update) | async-done | bytes 32784 | tf_op jit(solution)/shard_map/reduce_scatter | solution.py:74
  514.1 39.3 %psum.15 = f32[64]{0:T(128)S(1)} all-reduce(f32[64]{0:T(128)S(1)} %fusion.45), channel_id=1, replica_groups=mesh['seq'=8,'rep'=4] {'seq','rep'}, use_global_device_ids=true, to_apply=%region_12.15 | all-reduce | flops 64 | bytes 512 | tf_op jit(solution)/shard_map/psum | solution.py:78
  (134 shorter events, 115.0 us)
Async XLA Ops:
  6.5 236.4 %reduce-scatter.6.cloned.1.call-start = ((), (), s32[]{:S(2)}) async-start(), calls=%async_computation.4 | async-start | bytes 1179648 | tf_op jit(solution)/shard_map/reduce_scatter | solution.py:64
  13.0 158.3 %copy-start.1 = (s32[64]{0:T(128)S(1)}, s32[64]{0:T(128)}, u32[]{:S(2)}) copy-start(s32[64]{0:T(128)} %param.14) | copy-start | bytes 772
  171.3 4.7 copy-start
  176.0 157.9 %reduce-scatter.4.cloned.1.call-start = ((), (), s32[]{:S(2)}) async-start(), calls=%async_computation.3 | async-start | bytes 4718592 | tf_op jit(solution)/shard_map/reduce_scatter | solution.py:63
  182.8 330.5 %reduce-scatter.8.cloned.1.call-start = ((), (), s32[]{:S(2)}) async-start(), calls=%async_computation.5 | async-start | bytes 163840 | tf_op jit(solution)/shard_map/reduce_scatter | solution.py:74
Sparse Core Ops, SparseCore 0:
  176.1 66.8 reduce-scatter.5
  246.6 87.2 reduce-scatter.3
  494.0 19.2 reduce-scatter.7
where the time goes:
time: 564 us; the launch traced here: 561 us
  waiting for transfers between devices  144 us (26%)
  matrix products  116 us (21%)
  other arithmetic  114 us (20%)
  blocking collectives  94.6 us (17%)
  local copies, waits for them, and re-layouts  39.5 us (7%)
  loops' own time  36.8 us (7%)
  between operations  16.5 us (3%)
    dot_general x16, matrix products, one_head(): counted = jnp.dot(gradient, count_table, preferred_element_type=jnp.float32)  97.2 us
    reduce_scatter x1, waiting for transfers between devices, on_device(): lax.psum_scatter(local_grams, 'seq', scatter_dimension=0, tiled=True)  90 us
    another operation x14, other arithmetic, solve_queries(): factor = jnp.linalg.cholesky(gram_sum)  69.2 us
    another operation x5, other arithmetic, solve_queries(): jax.scipy.linalg.cho_solve((factor, True), chosen.T).astype(jnp.bfloat16)  39.9 us
    psum x1, blocking collectives, on_device(): norm_sum = lax.psum(partial_value, ('seq', 'rep')) / token_count  39.3 us
    another operation x1, loops' own time, build_sketches(): return lax.map(one_head, jnp.arange(head_count, dtype=jnp.int32))  36.7 us
    reduce_scatter x1, waiting for transfers between devices, on_device(): lax.psum_scatter(local_chosen, 'seq', scatter_dimension=0, tiled=True)  34.9 us
    all_gather x1, blocking collectives, on_device(): solved_all = lax.all_gather(solved, 'seq', axis=0, tiled=True)  31.4 us
  transfers between devices with their start and end apart: 3, of which 3 were waited for; matrix products, arithmetic and copies ran while one was open for 1% of the time, Pallas kernels for 0%

commit v1 on v0

v1 whole, which is shorter than its diff:
```python
import functools
import math

import jax
import jax.numpy as jnp
from jax import lax
from jax.experimental import pallas as pl
from jax.experimental.pallas import tpu as pltpu
from jax.sharding import PartitionSpec as P

ridge_shift = 0.25
norm_floor = 1e-06
NT = (((1,), (1,)), ((), ()))
TN = (((0,), (0,)), ((), ()))


def exact_dot(a, b, dims=(((1,), (0,)), ((), ()))):
    return lax.dot_general(
        a, b, dims, precision=lax.Precision.HIGHEST, preferred_element_type=jnp.float32
    )


def spd_inverse(mats):
    size = mats[0].shape[0]
    lane = lax.broadcasted_iota(jnp.int32, (1, size), 1)
    row8 = lax.broadcasted_iota(jnp.int32, (8, 1), 0)

    def pivots(_, mats):
        mats = list(mats)
        for k in range(8):
            for i, m in enumerate(mats):
                row, col = m[k : k + 1, :], m[:, k : k + 1]
                inv = 1.0 / row[:, k : k + 1]
                scaled = jnp.where(lane == k, inv, row * inv)
                new = jnp.where(lane == k, 0.0, m) - col * scaled
                top = jnp.where(row8 == k, scaled, new[:8])
                mats[i] = jnp.concatenate([top, new[8:]], axis=0)
        return tuple(
            pltpu.roll(jnp.concatenate([m[8:], m[:8]], axis=0), size - 8, 1) for m in mats
        )

    return lax.fori_loop(0, size // 8, pivots, tuple(mats))


def solve_rows(grams, rows):
    half = grams[0].shape[0] // 2
    inv_a = spd_inverse([g[:half, :half] for g in grams])
    cross = [g[:half, half:] for g in grams]
    w = [exact_dot(ia, b) for ia, b in zip(inv_a, cross)]
    inv_s = spd_inverse(
        [g[half:, half:] - exact_dot(b, wi, TN) for g, b, wi in zip(grams, cross, w)]
    )
    out = []
    for r, ia, wi, si in zip(rows, inv_a, w, inv_s):
        second = exact_dot(r[:, half:] - exact_dot(r[:, :half], wi), si)
        first = exact_dot(r[:, :half], ia) - exact_dot(second, wi, NT)
        out.append(jnp.concatenate([first, second], axis=1))
    return out


def sketch_kernel(scale, grad_ref, out_ref, codes_ref, mask_ref, hits_ref, sk_ref, gram_ref, ch_ref):
    head = pl.program_id(0)
    width = out_ref.shape[1]
    depth = grad_ref.shape[1]
    codes = codes_ref[pl.ds(head, 1), :]
    bucket = (codes % width).astype(jnp.float32).astype(jnp.bfloat16)
    sign = (1 - 2 * (codes // width)).astype(jnp.float32).astype(jnp.bfloat16)
    want = lax.broadcasted_iota(jnp.int32, (width, depth), 0).astype(jnp.float32).astype(jnp.bfloat16)
    table = jnp.where(bucket == want, sign, jnp.bfloat16(0))
    hashed = lax.dot_general(grad_ref[...], table, NT, preferred_element_type=jnp.float32)
    sketch = (out_ref[...].astype(jnp.float32) * hashed * scale).astype(jnp.bfloat16)
    sk_ref[...] = sketch
    gram_ref[0] = lax.dot_general(
        sketch * mask_ref[...], sketch, TN, preferred_element_type=jnp.float32
    )
    ch_ref[0] = jnp.dot(hits_ref[...], sketch, preferred_element_type=jnp.float32)


def sketch_all(outputs, gradient, codes, mask_col, hits):
    heads, depth = codes.shape
    rows, cols = outputs.shape
    width = cols // heads
    queries = hits.shape[0]
    whole = lambda h: (0, 0)
    once = pl.Buffered(1)

    return pl.pallas_call(
        functools.partial(sketch_kernel, math.sqrt(width / depth)),
        grid=(heads,),
        in_specs=[
            pl.BlockSpec((rows, depth), whole, pipeline_mode=once),
            pl.BlockSpec((rows, width), lambda h: (0, h)),
            pl.BlockSpec((heads, depth), whole, pipeline_mode=once),
            pl.BlockSpec((rows, 1), whole, pipeline_mode=once),
            pl.BlockSpec((queries, rows), whole, pipeline_mode=once),
        ],
        out_specs=[
            pl.BlockSpec((rows, width), lambda h: (0, h)),
            pl.BlockSpec((1, width, width), lambda h: (h, 0, 0)),
            pl.BlockSpec((1, queries, width), lambda h: (h, 0, 0)),
        ],
        out_shape=[
            jax.ShapeDtypeStruct((rows, cols), jnp.bfloat16),
            jax.ShapeDtypeStruct((heads, width, width), jnp.float32),
            jax.ShapeDtypeStruct((heads, queries, width), jnp.float32),
        ],
        compiler_params=pltpu.CompilerParams(vmem_limit_bytes=40 << 20),
        cost_estimate=pl.CostEstimate(
            flops=2 * rows * depth * cols, bytes_accessed=4 * rows * cols, transcendentals=0
        ),
        name="sketch",
    )(gradient, outputs, codes, mask_col, hits)


def solve_kernel(count_ref, gram_ref, ch_ref, out_ref):
    width = gram_ref.shape[1]
    diag = lax.broadcasted_iota(jnp.int32, (width, width), 0) == lax.broadcasted_iota(
        jnp.int32, (width, width), 1
    )
    ridge = jnp.where(diag, ridge_shift, 0.0)
    slots = range(gram_ref.shape[0])
    grams = [gram_ref[i] / count_ref[0, 0] + ridge for i in slots]
    for i, solved in enumerate(solve_rows(grams, [ch_ref[i] for i in slots])):
        out_ref[i] = solved.astype(jnp.bfloat16)


def solve_all(count, grams, chosen):
    vmem = pl.BlockSpec(memory_space=pltpu.VMEM)
    return pl.pallas_call(
        solve_kernel,
        in_specs=[pl.BlockSpec(memory_space=pltpu.SMEM), vmem, vmem],
        out_specs=vmem,
        out_shape=jax.ShapeDtypeStruct(chosen.shape, jnp.bfloat16),
        name="solve",
    )(count.reshape(1, 1), grams, chosen)


def on_device(head_out, grad_out, hash_codes, loss_mask, query_ids):
    tok_rows = loss_mask.shape[0]
    out_rows = tok_rows // lax.axis_size("rep")
    local_count = jnp.sum(loss_mask.astype(jnp.float32))
    token_count = lax.psum(local_count, "seq") + 1.0
    first_row = lax.axis_index("seq") * tok_rows
    query_hits = (
        query_ids[:, None] - first_row == jnp.arange(tok_rows, dtype=jnp.int32)[None, :]
    ).astype(jnp.bfloat16)
    sketches, local_grams, local_chosen = sketch_all(
        head_out[0], grad_out[0], hash_codes[0], loss_mask.astype(jnp.bfloat16)[:, None], query_hits
    )
    own_grams = lax.psum_scatter(local_grams, "seq", scatter_dimension=0, tiled=True)
    own_chosen = lax.psum_scatter(local_chosen, "seq", scatter_dimension=0, tiled=True)
    solved = solve_all(token_count, own_grams, own_chosen)
    solved_all = lax.all_gather(solved, "seq", axis=0, tiled=True)
    heads, queries, width = solved_all.shape
    score_sum = jnp.einsum(
        "thk,hqk->tq",
        sketches.reshape(tok_rows, heads, width),
        solved_all,
        preferred_element_type=jnp.float32,
    )
    contrib = lax.psum_scatter(score_sum, "rep", scatter_dimension=0, tiled=True)
    row_start = lax.axis_index("rep") * out_rows
    mask_rows = lax.dynamic_slice_in_dim(loss_mask, row_start, out_rows, 0).astype(jnp.float32)
    partial_value = jnp.sum(mask_rows[:, None] * contrib * contrib, 0)
    norm_sum = lax.psum(partial_value, ("seq", "rep")) / token_count
    return contrib / jnp.sqrt(norm_sum + norm_floor)


def solution(mesh):
    placed = (P("rep", "seq", None), P("rep", "seq", None), P("rep", None, None), P("seq"), P())
    return jax.shard_map(
        on_device, mesh=mesh, in_specs=placed, out_specs=P(("seq", "rep"), None), check_vma=False
    )
```

time: 564 us -> 333 us (0.59)
  matrix products: 116 us -> 4.22 us
  other arithmetic: 114 us -> 4.43 us
  Pallas kernels: 0 us -> 55.7 us
  loops' own time: 36.8 us -> 0 us
  local copies, waits for them, and re-layouts: 39.5 us -> 7 us
  waiting for transfers between devices: 144 us -> 152 us
    another operation x22 -> x0, other arithmetic: 109 us -> none  [the longest x14 69.2 us: solve_queries(): factor = jnp.linalg.cholesky(gram_sum)]
    dot_general x19 -> x1, matrix products: 112 us -> 4.22 us  [on_device(): jnp.einsum('thk,hqk->tq', sketches.reshape(tok_rows, heads, width), solve...]
    pallas_call x0 -> x2, Pallas kernels: none -> 55.7 us  [the longest x1 29.2 us: solve_all(): pl.pallas_call(solve_kernel, in_specs=[pl.BlockSpec(memory_space=pltpu.SM...]
    another operation x3 -> x0, loops' own time: 36.8 us -> none  [the longest x1 36.7 us: build_sketches(): return lax.map(one_head, jnp.arange(head_count, dtype=jnp.int32))]
    dynamic_slice x32 -> x0, local copies, waits for them, and re-layouts: 24 us -> none  [the longest x16 15.2 us: one_head(): head_codes = codes[head_index]]
    another operation x19 -> x0, local copies, waits for them, and re-layouts: 7.86 us -> none  [the longest x15 7.81 us: solve_queries(): jax.scipy.linalg.cho_solve((factor, True), chosen.T).astype(jnp.bfloat16)]
    reduce_scatter x1, waiting for transfers between devices: 34.9 us -> 41.3 us  [on_device(): lax.psum_scatter(local_chosen, 'seq', scatter_dimension=0, tiled=True)]
  transfers between devices with their start and end apart: 3 -> 3, of which waited for: 3 -> 3; matrix products, arithmetic and copies ran while one was open for 1% -> 0% of each run, Pallas kernels for 0% -> 0%
where the time goes in v1:
time: 333 us; the launch traced here: 332 us
  waiting for transfers between devices  152 us (46%)
  blocking collectives  94.8 us (28%)
  Pallas kernels  55.7 us (17%)
  between operations  13.8 us (4%)
  local copies, waits for them, and re-layouts  7 us (2%)
  other arithmetic  4.43 us (1%)
  matrix products  4.22 us (1%)
    reduce_scatter x1, waiting for transfers between devices, on_device(): lax.psum_scatter(local_grams, 'seq', scatter_dimension=0, tiled=True)  90.9 us
    reduce_scatter x1, waiting for transfers between devices, on_device(): lax.psum_scatter(local_chosen, 'seq', scatter_dimension=0, tiled=True)  41.3 us
    psum x1, blocking collectives, on_device(): norm_sum = lax.psum(partial_value, ('seq', 'rep')) / token_count  39.3 us
    all_gather x1, blocking collectives, on_device(): solved_all = lax.all_gather(solved, 'seq', axis=0, tiled=True)  31.6 us
    pallas_call x1, Pallas kernels, solve_all(): pl.pallas_call(solve_kernel, in_specs=[pl.BlockSpec(memory_space=pltpu.SM...  29.2 us
    pallas_call x1, Pallas kernels, sketch_all(): pl.pallas_call(functools.partial(sketch_kernel, math.sqrt(width / depth))...  26.5 us
    psum x1, blocking collectives, on_device(): token_count = lax.psum(local_count, 'seq') + 1.0  23.9 us
    reduce_scatter x1, waiting for transfers between devices, on_device(): lax.psum_scatter(score_sum, 'rep', scatter_dimension=0, tiled=True)  19.3 us
  transfers between devices with their start and end apart: 3, of which 3 were waited for; matrix products, arithmetic and copies ran while one was open for 0% of the time, Pallas kernels for 0%

profile of v1, /device:TPU:0, one launch (start us, length us, event | category | flops | bytes accessed | tf_op | source)
XLA Modules:
  0.0 332.3 jit_solution(3015539247869904539)
XLA Ops:
  6.5 0.7 broadcast_subtract_fusion
  7.2 0.1 fusion.6.hits_ref
  7.3 0.7 convert_element_type.12
  8.0 0.1 broadcast_in_dim.3.mask_ref
  8.1 2.0 copy-done.1
  10.2 0.9 copy-done.2
  11.1 26.5 %sketch.1 = (bf16[512,4096]{1,0:T(8,128)(2,1)S(1)}, f32[16,256,256]{2,1,0:T(8,128)S(1)}, f32[16,64,256]{2,1,0:T(8,128)}) custom-call(bf16[512,3584]{1,0:T(8,128)(2,1)S(1)} %bitcast.13, bf16[512,4096]{1,0:T(8,128)(2,1)} %bitcast.16, s32[16,3584]{1,0:T(8,128)S(1)} %bitcast.14, bf16[512,1]{1,0:T(8,128)(2,1)S(1)} %broadcast_in_dim.3.mask_ref, ...), custom_call_target="tpu_custom_call" | custom-call | flops 15032385536 | bytes 8388608 | tf_op jit(solution)/shard_map/sketch/pallas_call | solution.py:87
  37.6 2.0 copy-done
  39.5 1.9 copy-done.3
  41.5 0.0 reduce-scatter.4.cloned.1.call-start
  41.5 0.7 reduce-scatter.4.cloned.1.call-update
  42.2 0.0 reduce-scatter.8.cloned.1.call-start
  42.3 0.6 convert_reduce_fusion
  42.9 23.9 %psum.14 = f32[]{:T(128)} all-reduce(f32[]{:T(128)} %convert_reduce_fusion), channel_id=1, replica_groups=mesh['seq'=8,'rep'=4] {'seq'}, use_global_device_ids=true, to_apply=%region_1.0 | all-reduce | flops 1 | bytes 8 | tf_op jit(solution)/shard_map/psum | solution.py:142
  67.5 41.3 %reduce-scatter.6.cloned.1.call-done.ch_ref = f32[2,64,256]{2,1,0:T(8,128)} async-done(((f32[16,64,256]{2,1,0:T(8,128)}), f32[2,64,256]{2,1,0:T(8,128)}) %reduce-scatter.6.cloned.1.call-update) | async-done | bytes 131088 | tf_op jit(solution)/shard_map/reduce_scatter | solution.py:151
  108.8 90.9 %reduce-scatter.4.cloned.1.call-done.gram_ref = f32[2,256,256]{2,1,0:T(8,128)} async-done(((f32[16,256,256]{2,1,0:T(8,128)}), f32[2,256,256]{2,1,0:T(8,128)}) %reduce-scatter.4.cloned.1.call-update) | async-done | bytes 524304 | tf_op jit(solution)/shard_map/reduce_scatter | solution.py:150
  199.7 29.2 %solve.1 = bf16[2,64,256]{2,1,0:T(8,128)(2,1)} custom-call(f32[1,1]{1,0:T(1,128)} %bitcast.3.count_ref, f32[2,256,256]{2,1,0:T(8,128)} %reduce-scatter.4.cloned.1.call-done.gram_ref, f32[2,64,256]{2,1,0:T(8,128)} %reduce-scatter.6.cloned.1.call-done.ch_ref), custom_call_target="tpu_custom_call" | custom-call | tf_op jit(solution)/shard_map/solve/pallas_call | solution.py:129
  228.8 31.6 %all_gather.3 = bf16[16,64,256]{2,1,0:T(8,128)(2,1)S(1)} all-gather(bf16[2,64,256]{2,1,0:T(8,128)(2,1)} %solve.1), channel_id=1, replica_groups=mesh['seq'=8,'rep'=4] {'seq'}, dimensions={0}, use_global_device_ids=true | all-gather | bytes 589824 | tf_op jit(solution)/shard_map/all_gather | solution.py:153
  260.4 4.2 %fusion.3 = f32[512,64]{0,1:T(8,128)} fusion(bf16[16,64,256]{2,1,0:T(8,128)(2,1)S(1)} %all_gather.3, bf16[64,16,8,256]{3,2,1,0:T(8,128)(2,1)} %bitcast.15), kind=kOutput, calls=%fused_computation.3 | convolution fusion | flops 268435456 | bytes 4849664 | tf_op jit(solution)/shard_map/thk,hqk->tq/dot_general | solution.py:155
  264.7 0.1 dynamic-slice_convert_fusion
  264.8 19.3 %reduce-scatter.8.cloned.1.call-done = f32[128,64]{0,1:T(8,128)} async-done(((f32[512,64]{0,1:T(8,128)}), f32[128,64]{0,1:T(8,128)}) %reduce-scatter.8.cloned.1.call-update) | async-done | bytes 32784 | tf_op jit(solution)/shard_map/reduce_scatter | solution.py:161
  284.1 0.9 fusion.7
  284.9 39.3 %psum.15 = f32[64]{0:T(128)S(1)} all-reduce(f32[64]{0:T(128)S(1)} %fusion.7), channel_id=1, replica_groups=mesh['seq'=8,'rep'=4] {'seq','rep'}, use_global_device_ids=true, to_apply=%region_6.0 | all-reduce | flops 64 | bytes 512 | tf_op jit(solution)/shard_map/psum | solution.py:165
  324.3 1.5 broadcast_divide_fusion
  (10 shorter events, 0.1 us)
Async XLA Ops:
  6.5 102.2 %reduce-scatter.6.cloned.1.call-start = ((), (), s32[]{:S(2)}) async-start(), calls=%async_computation.4 | async-start | bytes 1179648 | tf_op jit(solution)/shard_map/reduce_scatter | solution.py:151
  8.1 2.0 copy-start.1
  10.2 0.9 copy-start.2
  37.6 2.0 copy-start
  39.5 1.9 copy-start.3
  41.5 0.8 copy-start.4
  41.5 158.2 %reduce-scatter.4.cloned.1.call-start = ((), (), s32[]{:S(2)}) async-start(), calls=%async_computation.3 | async-start | bytes 4718592 | tf_op jit(solution)/shard_map/reduce_scatter | solution.py:150
  42.2 241.8 %reduce-scatter.8.cloned.1.call-start = ((), (), s32[]{:S(2)}) async-start(), calls=%async_computation.5 | async-start | bytes 163840 | tf_op jit(solution)/shard_map/reduce_scatter | solution.py:161
Sparse Core Ops, SparseCore 0:
  41.6 67.1 reduce-scatter.5
  112.4 87.2 reduce-scatter.3
  264.8 19.2 reduce-scatter.7

commit v2 on v0

v2 whole, which is shorter than its diff:
```python
import functools
import math

import jax
import jax.numpy as jnp
from jax import lax
from jax.experimental import pallas as pl
from jax.experimental.pallas import tpu as pltpu
from jax.sharding import PartitionSpec as P

ridge_shift = 0.25
norm_floor = 1e-06
NT = (((1,), (1,)), ((), ()))
TN = (((0,), (0,)), ((), ()))


def exact_dot(a, b, dims=(((1,), (0,)), ((), ()))):
    return lax.dot_general(
        a, b, dims, precision=lax.Precision.HIGHEST, preferred_element_type=jnp.float32
    )


def spd_inverse(mats):
    size = mats[0].shape[0]
    lane = lax.broadcasted_iota(jnp.int32, (1, size), 1)
    row8 = lax.broadcasted_iota(jnp.int32, (8, 1), 0)

    def pivots(_, mats):
        mats = list(mats)
        for k in range(8):
            for i, m in enumerate(mats):
                row, col = m[k : k + 1, :], m[:, k : k + 1]
                inv = 1.0 / row[:, k : k + 1]
                scaled = jnp.where(lane == k, inv, row * inv)
                new = jnp.where(lane == k, 0.0, m) - col * scaled
                top = jnp.where(row8 == k, scaled, new[:8])
                mats[i] = jnp.concatenate([top, new[8:]], axis=0)
        return tuple(
            pltpu.roll(jnp.concatenate([m[8:], m[:8]], axis=0), size - 8, 1) for m in mats
        )

    return lax.fori_loop(0, size // 8, pivots, tuple(mats))


def solve_rows(blocks, rows):
    half = blocks[0][0].shape[0]
    inv_a = spd_inverse([a for a, _, _ in blocks])
    w = [exact_dot(ia, b) for ia, (_, b, _) in zip(inv_a, blocks)]
    inv_s = spd_inverse([c - exact_dot(b, wi, TN) for (_, b, c), wi in zip(blocks, w)])
    out = []
    for r, ia, wi, si in zip(rows, inv_a, w, inv_s):
        second = exact_dot(r[:, half:] - exact_dot(r[:, :half], wi), si)
        first = exact_dot(r[:, :half], ia) - exact_dot(second, wi, NT)
        out.append(jnp.concatenate([first, second], axis=1))
    return out


def peer_copy(src, dst, send, recv, axis, index):
    return pltpu.make_async_remote_copy(
        src_ref=src,
        dst_ref=dst,
        send_sem=send,
        recv_sem=recv,
        device_id={axis: index},
        device_id_type=pl.DeviceIdType.MESH,
    )


def others(axis, body):
    size, me = lax.axis_size(axis), lax.axis_index(axis)

    def step(s, carry):
        body(lax.rem(me + 1 + s, size))
        return carry

    lax.fori_loop(0, size - 1, step, 0)


def whole_kernel(
    scale,
    own_heads,
    grad_ref,
    cols_ref,
    codes_ref,
    mask_ref,
    ids_ref,
    out_ref,
    sk_ref,
    hits_ref,
    gram_stage,
    gram_in,
    ch_stage,
    ch_in,
    solved_ref,
    score_ref,
    score_in,
    rep_norm,
    seq_norm,
    gram_sems,
    ch_sems,
    solved_sems,
    score_sems,
    rep_sems,
    seq_sems,
):
    n_seq, n_rep = lax.axis_size("seq"), lax.axis_size("rep")
    me, layer = lax.axis_index("seq"), lax.axis_index("rep")
    rows, depth = grad_ref.shape
    width = cols_ref.shape[1] // codes_ref.shape[0]
    half = width // 2
    out_rows = out_ref.shape[0]

    barrier = pltpu.get_barrier_semaphore()
    for axis in ("seq", "rep"):
        others(
            axis,
            lambda peer, axis=axis: pl.semaphore_signal(
                barrier, inc=1, device_id={axis: peer}, device_id_type=pl.DeviceIdType.MESH
            ),
        )

    mask = mask_ref[...]
    count = jnp.sum(mask, axis=0, keepdims=True)
    token = lax.broadcasted_iota(jnp.int32, (ids_ref.shape[0], rows), 1)
    hits_ref[...] = jnp.where(ids_ref[...] - me * rows == token, 1.0, 0.0).astype(jnp.bfloat16)

    def sketch_head(head, gram_to, ch_to):
        codes = codes_ref[pl.ds(head, 1), :]
        flipped = codes >= width
        bucket = jnp.where(flipped, codes - width, codes)
        bucket = bucket.astype(jnp.float32).astype(jnp.bfloat16)
        sign = jnp.where(flipped, -1.0, 1.0).astype(jnp.bfloat16)
        want = lax.broadcasted_iota(jnp.int32, (width, depth), 0)
        want = want.astype(jnp.float32).astype(jnp.bfloat16)
        table = jnp.where(bucket == want, sign, jnp.bfloat16(0))
        hashed = lax.dot_general(grad_ref[...], table, NT, preferred_element_type=jnp.float32)
        span = pl.ds(pl.multiple_of(head * width, width), width)
        sketch = (cols_ref[:, span].astype(jnp.float32) * hashed * scale).astype(jnp.bfloat16)
        sk_ref[:, span] = sketch
        gram = lax.dot_general(
            sketch * mask_ref[...].astype(jnp.bfloat16),
            sketch,
            TN,
            preferred_element_type=jnp.float32,
        )
        gram_to[:half, :width] = gram[:half]
        gram_to[:half, width:] = gram[half:, half:]
        gram_to[half:, :] = jnp.broadcast_to(count, (8, width + half))
        ch_to[...] = jnp.dot(
            hits_ref[...], sketch, preferred_element_type=jnp.float32
        ).astype(jnp.bfloat16)

    def gram_copy(peer, slot, source):
        return peer_copy(
            gram_stage.at[peer, slot],
            gram_in.at[source, slot],
            gram_sems.at[0, peer, slot],
            gram_sems.at[1, source, slot],
            "seq",
            peer,
        )

    def ch_copy(peer, slot, source):
        return peer_copy(
            ch_stage.at[peer, slot],
            ch_in.at[source, slot],
            ch_sems.at[0, peer, slot],
            ch_sems.at[1, source, slot],
            "seq",
            peer,
        )

    pl.semaphore_wait(barrier, n_seq + n_rep - 2)

    def make_and_send(peer):
        def one(slot, carry):
            sketch_head(
                peer * own_heads + slot, gram_stage.at[peer, slot], ch_stage.at[peer, slot]
            )
            gram_copy(peer, slot, me).start()
            ch_copy(peer, slot, me).start()
            return carry

        lax.fori_loop(0, own_heads, one, 0)

    def make_own(slot, carry):
        sketch_head(me * own_heads + slot, gram_in.at[me, slot], ch_in.at[me, slot])
        return carry

    others("seq", make_and_send)
    lax.fori_loop(0, own_heads, make_own, 0)

    def arrived(peer):
        for slot in range(own_heads):
            gram_copy(peer, slot, peer).wait_recv()
            ch_copy(peer, slot, peer).wait_recv()

    others("seq", arrived)

    diag = lax.broadcasted_iota(jnp.int32, (half, half), 0) == lax.broadcasted_iota(
        jnp.int32, (half, half), 1
    )
    ridge = jnp.where(diag, ridge_shift, 0.0)
    packs, chosen = [], []
    for slot in range(own_heads):
        total, picked = gram_in[0, slot], ch_in[0, slot].astype(jnp.float32)
        for source in range(1, n_seq):
            total = total + gram_in[source, slot]
            picked = picked + ch_in[source, slot].astype(jnp.float32)
        packs.append(total)
        chosen.append(picked)
    tokens = packs[0][half : half + 1, :1] + 1.0
    blocks = [
        (
            p[:half, :half] / tokens + ridge,
            p[:half, half:width] / tokens,
            p[:half, width:] / tokens + ridge,
        )
        for p in packs
    ]
    mine = pl.ds(pl.multiple_of(me * own_heads * width, width), own_heads * width)
    solved = solve_rows(blocks, chosen)
    solved_ref[:, mine] = jnp.concatenate(solved, axis=1).astype(jnp.bfloat16)

    def solved_copy(peer, source):
        span = pl.ds(pl.multiple_of(source * own_heads * width, width), own_heads * width)
        return peer_copy(
            solved_ref.at[:, span],
            solved_ref.at[:, span],
            solved_sems.at[0, peer],
            solved_sems.at[1, source],
            "seq",
            peer,
        )

    others("seq", lambda peer: solved_copy(peer, me).start())
    others("seq", lambda peer: solved_copy(peer, peer).wait_recv())
    score_ref[...] = lax.dot_general(
        sk_ref[...], solved_ref[...], NT, preferred_element_type=jnp.float32
    )

    def score_copy(peer, source):
        return peer_copy(
            score_ref.at[pl.ds(pl.multiple_of(peer * out_rows, out_rows), out_rows)],
            score_in.at[source],
            score_sems.at[0, peer],
            score_sems.at[1, source],
            "rep",
            peer,
        )

    own_rows = pl.ds(pl.multiple_of(layer * out_rows, out_rows), out_rows)
    others("rep", lambda peer: score_copy(peer, layer).start())
    score_in[layer] = score_ref[own_rows, :]
    others("rep", lambda peer: score_copy(peer, peer).wait_recv())
    contrib = score_in[0]
    for source in range(1, n_rep):
        contrib = contrib + score_in[source]

    def norm_copy(buf, sems, axis, peer, here, source):
        return peer_copy(
            buf.at[here], buf.at[source], sems.at[0, peer], sems.at[1, source], axis, peer
        )

    squares = jnp.sum(mask_ref[own_rows, :] * contrib * contrib, axis=0, keepdims=True)
    for buf, sems, axis, here, size in (
        (rep_norm, rep_sems, "rep", layer, n_rep),
        (seq_norm, seq_sems, "seq", me, n_seq),
    ):
        buf[here] = jnp.broadcast_to(squares, buf.shape[1:])
        others(axis, lambda peer: norm_copy(buf, sems, axis, peer, here, here).start())
        others(axis, lambda peer: norm_copy(buf, sems, axis, peer, here, peer).wait_recv())
        squares = buf[0, :1]
        for source in range(1, size):
            squares = squares + buf[source, :1]
    out_ref[...] = contrib / jnp.sqrt(squares / tokens + norm_floor)

    def sent(peer):
        for slot in range(own_heads):
            gram_copy(peer, slot, me).wait_send()
            ch_copy(peer, slot, me).wait_send()
        solved_copy(peer, me).wait_send()
        norm_copy(seq_norm, seq_sems, "seq", peer, me, me).wait_send()

    def sent_rep(peer):
        score_copy(peer, layer).wait_send()
        norm_copy(rep_norm, rep_sems, "rep", peer, layer, layer).wait_send()

    others("seq", sent)
    others("rep", sent_rep)


def on_device(head_out, grad_out, hash_codes, loss_mask, query_ids):
    outputs, gradient, codes = head_out[0], grad_out[0], hash_codes[0]
    n_seq, n_rep = lax.axis_size("seq"), lax.axis_size("rep")
    heads, depth = codes.shape
    rows, cols = outputs.shape
    width, own_heads = cols // heads, heads // n_seq
    queries = query_ids.shape[0]
    out_rows = rows // n_rep
    pack = (n_seq, own_heads, width // 2 + 8, width + width // 2)
    picked = (n_seq, own_heads, queries, width)
    vmem = pl.BlockSpec(memory_space=pltpu.VMEM)
    f32, bf16, dma = jnp.float32, jnp.bfloat16, pltpu.SemaphoreType.DMA
    return pl.pallas_call(
        functools.partial(whole_kernel, math.sqrt(width / depth), own_heads),
        in_specs=[vmem] * 5,
        out_specs=vmem,
        out_shape=jax.ShapeDtypeStruct((out_rows, queries), f32),
        scratch_shapes=[
            pltpu.VMEM((rows, cols), bf16),
            pltpu.VMEM((queries, rows), bf16),
            pltpu.VMEM(pack, f32),
            pltpu.VMEM(pack, f32),
            pltpu.VMEM(picked, bf16),
            pltpu.VMEM(picked, bf16),
            pltpu.VMEM((queries, cols), bf16),
            pltpu.VMEM((rows, queries), f32),
            pltpu.VMEM((n_rep, out_rows, queries), f32),
            pltpu.VMEM((n_rep, 8, queries), f32),
            pltpu.VMEM((n_seq, 8, queries), f32),
            dma((2, n_seq, own_heads)),
            dma((2, n_seq, own_heads)),
            dma((2, n_seq)),
            dma((2, n_rep)),
            dma((2, n_rep)),
            dma((2, n_seq)),
        ],
        compiler_params=pltpu.CompilerParams(
            collective_id=0, has_side_effects=True, vmem_limit_bytes=56 << 20
        ),
        name="attribute",
    )(
        gradient,
        outputs,
        codes,
        loss_mask.astype(f32)[:, None],
        query_ids[:, None],
    )


def solution(mesh):
    placed = (P("rep", "seq", None), P("rep", "seq", None), P("rep", None, None), P("seq"), P())
    return jax.shard_map(
        on_device, mesh=mesh, in_specs=placed, out_specs=P(("seq", "rep"), None), check_vma=False
    )
```

time: 564 us -> 153 us (0.27)
  Pallas kernels: 0 us -> 149 us
  waiting for transfers between devices: 144 us -> 0 us
  matrix products: 116 us -> 0 us
  other arithmetic: 114 us -> 0.68 us
  blocking collectives: 94.6 us -> 0 us
  loops' own time: 36.8 us -> 0 us
  local copies, waits for them, and re-layouts: 39.5 us -> 3.74 us
  between operations: 16.5 us -> 0.01 us
    pallas_call x0 -> x1, Pallas kernels: none -> 149 us  [on_device(): pl.pallas_call(functools.partial(whole_kernel, math.sqrt(width / depth),...]
    reduce_scatter x3 -> x0, waiting for transfers between devices: 144 us -> none  [the longest x1 90 us: on_device(): lax.psum_scatter(local_grams, 'seq', scatter_dimension=0, tiled=True)]
    dot_general x19 -> x0, matrix products: 112 us -> none  [the longest x16 97.2 us: one_head(): counted = jnp.dot(gradient, count_table, preferred_element_type=jnp.float32)]
    another operation x22 -> x0, other arithmetic: 109 us -> none  [the longest x14 69.2 us: solve_queries(): factor = jnp.linalg.cholesky(gram_sum)]
    psum x2 -> x0, blocking collectives: 63.3 us -> none  [the longest x1 39.3 us: on_device(): norm_sum = lax.psum(partial_value, ('seq', 'rep')) / token_count]
    another operation x3 -> x0, loops' own time: 36.8 us -> none  [the longest x1 36.7 us: build_sketches(): return lax.map(one_head, jnp.arange(head_count, dtype=jnp.int32))]
    all_gather x1 -> x0, blocking collectives: 31.4 us -> none  [on_device(): solved_all = lax.all_gather(solved, 'seq', axis=0, tiled=True)]
    dynamic_slice x32 -> x0, local copies, waits for them, and re-layouts: 24 us -> none  [the longest x16 15.2 us: one_head(): head_codes = codes[head_index]]
  transfers between devices with their start and end apart: 3 -> 0, of which waited for: 3 -> 0; matrix products, arithmetic and copies ran while one was open for 1% -> 0% of each run, Pallas kernels for 0% -> 0%
where the time goes in v2:
time: 153 us
  Pallas kernels  149 us (97%)
  local copies, waits for them, and re-layouts  3.74 us (2%)
    pallas_call x1, Pallas kernels, on_device(): pl.pallas_call(functools.partial(whole_kernel, math.sqrt(width / depth),...  149 us

profile of v2, /device:TPU:0, one launch (start us, length us, event | category | flops | bytes accessed | tf_op | source)
XLA Modules:
  0.0 153.1 jit_solution(4638490511713323281)
XLA Ops:
  0.0 0.7 convert_element_type.3
  0.7 1.4 copy.9.ids_ref
  2.0 0.8 copy.8.mask_ref
  2.9 148.7 %attribute.1 = f32[128,64]{1,0:T(8,128)} custom-call(bf16[512,3584]{1,0:T(8,128)(2,1)} %bitcast.6, bf16[512,4096]{1,0:T(8,128)(2,1)} %bitcast.5, s32[16,3584]{1,0:T(8,128)} %bitcast.7, f32[512,1]{1,0:T(8,128)} %copy.8.mask_ref, s32[64,1]{1,0:T(8,128)} %copy.9.ids_ref), custom_call_target="tpu_custom_call" | custom-call | tf_op jit(solution)/shard_map/attribute/pallas_call | solution.py:305
  151.6 1.5 %copy.10 = f32[128,64]{0,1:T(8,128)} copy(f32[128,64]{1,0:T(8,128)} %attribute.1) | data formatting | bytes 65536 | tf_op jit(solution)/shard_map/attribute/pallas_call | solution.py:305

commit v3 on v2

--- a/solution.py
+++ b/solution.py
@@ -26,18 +26,19 @@
     row8 = lax.broadcasted_iota(jnp.int32, (8, 1), 0)
 
     def pivots(_, mats):
-        mats = list(mats)
+        panels = [m[:8] for m in mats]
         for k in range(8):
-            for i, m in enumerate(mats):
-                row, col = m[k : k + 1, :], m[:, k : k + 1]
+            for i, p in enumerate(panels):
+                row, col = p[k : k + 1, :], p[:, k : k + 1]
                 inv = 1.0 / row[:, k : k + 1]
                 scaled = jnp.where(lane == k, inv, row * inv)
-                new = jnp.where(lane == k, 0.0, m) - col * scaled
-                top = jnp.where(row8 == k, scaled, new[:8])
-                mats[i] = jnp.concatenate([top, new[8:]], axis=0)
-        return tuple(
-            pltpu.roll(jnp.concatenate([m[8:], m[:8]], axis=0), size - 8, 1) for m in mats
-        )
+                new = jnp.where(lane == k, 0.0, p) - col * scaled
+                panels[i] = jnp.where(row8 == k, scaled, new)
+        done = []
+        for m, p in zip(mats, panels):
+            rest = jnp.where(lane < 8, 0.0, m[8:]) - exact_dot(m[8:, :8], p)
+            done.append(pltpu.roll(jnp.concatenate([rest, p], axis=0), size - 8, 1))
+        return tuple(done)
 
     return lax.fori_loop(0, size // 8, pivots, tuple(mats))
 
@@ -88,14 +89,20 @@
     sk_ref,
     hits_ref,
     gram_stage,
+    gram_pair,
+    gram_sum,
     gram_in,
     ch_stage,
+    ch_pair,
+    ch_sum,
     ch_in,
     solved_ref,
     score_ref,
     score_in,
     rep_norm,
     seq_norm,
+    gram_pair_sems,
+    ch_pair_sems,
     gram_sems,
     ch_sems,
     solved_sems,
@@ -150,52 +157,84 @@
             hits_ref[...], sketch, preferred_element_type=jnp.float32
         ).astype(jnp.bfloat16)
 
-    def gram_copy(peer, slot, source):
-        return peer_copy(
-            gram_stage.at[peer, slot],
-            gram_in.at[source, slot],
-            gram_sems.at[0, peer, slot],
-            gram_sems.at[1, source, slot],
-            "seq",
-            peer,
-        )
-
-    def ch_copy(peer, slot, source):
-        return peer_copy(
-            ch_stage.at[peer, slot],
-            ch_in.at[source, slot],
-            ch_sems.at[0, peer, slot],
-            ch_sems.at[1, source, slot],
-            "seq",
-            peer,
-        )
+    chips = n_seq // 2
+    chip, side = me // 2, lax.rem(me, 2)
+    partner = me + 1 - 2 * side
+
+    def pair_copies(to, slot):
+        return [
+            peer_copy(
+                src.at[to, slot],
+                dst.at[to, slot],
+                sems.at[0, to, slot],
+                sems.at[1, to, slot],
+                "seq",
+                partner,
+            )
+            for src, dst, sems in (
+                (gram_stage, gram_pair, gram_pair_sems),
+                (ch_stage, ch_pair, ch_pair_sems),
+            )
+        ]
+
+    def owner_copies(to, slot, source):
+        return [
+            peer_copy(
+                src.at[to, slot],
+                dst.at[source, slot],
+                sems.at[0, to, slot],
+                sems.at[1, source, slot],
+                "seq",
+                2 * to + side,
+            )
+            for src, dst, sems in ((gram_sum, gram_in, gram_sems), (ch_sum, ch_in, ch_sems))
+        ]
 
     pl.semaphore_wait(barrier, n_seq + n_rep - 2)
 
-    def make_and_send(peer):
-        def one(slot, carry):
-            sketch_head(
-                peer * own_heads + slot, gram_stage.at[peer, slot], ch_stage.at[peer, slot]
-            )
-            gram_copy(peer, slot, me).start()
-            ch_copy(peer, slot, me).start()
+    def for_partner(i, carry):
+        to, slot = lax.rem(chip + 1 + i // own_heads, chips), lax.rem(i, own_heads)
+        head = (2 * to + 1 - side) * own_heads + slot
+        sketch_head(head, gram_stage.at[to, slot], ch_stage.at[to, slot])
+        for copy in pair_copies(to, slot):
+            copy.start()
+        return carry
+
+    def join(to, slot, gram_to, ch_to):
+        sketch_head((2 * to + side) * own_heads + slot, gram_to, ch_to)
+        for copy in pair_copies(to, slot):
+            copy.wait_recv()
+        gram_to[...] = gram_to[...] + gram_pair[to, slot]
+        both = ch_to[...].astype(jnp.float32) + ch_pair[to, slot].astype(jnp.float32)
+        ch_to[...] = both.astype(jnp.bfloat16)
+
+    def for_owner(i, carry):
+        to, slot = lax.rem(chip + 1 + i // own_heads, chips), lax.rem(i, own_heads)
+        join(to, slot, gram_sum.at[to, slot], ch_sum.at[to, slot])
+        for copy in owner_copies(to, slot, chip):
+            copy.start()
+        return carry
+
+    def for_me(slot, carry):
+        join(chip, slot, gram_in.at[chip, slot], ch_in.at[chip, slot])
+        return carry
+
+    def other_chips(body):
+        def step(i, carry):
+            to, slot = lax.rem(chip + 1 + i // own_heads, chips), lax.rem(i, own_heads)
+            body(to, slot)
             return carry
 
-        lax.fori_loop(0, own_heads, one, 0)
-
-    def make_own(slot, carry):
-        sketch_head(me * own_heads + slot, gram_in.at[me, slot], ch_in.at[me, slot])
-        return carry
-
-    others("seq", make_and_send)
-    lax.fori_loop(0, own_heads, make_own, 0)
-
-    def arrived(peer):
-        for slot in range(own_heads):
-            gram_copy(peer, slot, peer).wait_recv()
-            ch_copy(peer, slot, peer).wait_recv()
-
-    others("seq", arrived)
+        lax.fori_loop(0, (chips - 1) * own_heads, step, 0)
+
+    def arrived(to, slot):
+        for copy in owner_copies(to, slot, to):
+            copy.wait_recv()
+
+    lax.fori_loop(0, chips * own_heads, for_partner, 0)
+    lax.fori_loop(0, (chips - 1) * own_heads, for_owner, 0)
+    lax.fori_loop(0, own_heads, for_me, 0)
+    other_chips(arrived)
 
     diag = lax.broadcasted_iota(jnp.int32, (half, half), 0) == lax.broadcasted_iota(
         jnp.int32, (half, half), 1
@@ -204,7 +243,7 @@
     packs, chosen = [], []
     for slot in range(own_heads):
         total, picked = gram_in[0, slot], ch_in[0, slot].astype(jnp.float32)
-        for source in range(1, n_seq):
+        for source in range(1, chips):
             total = total + gram_in[source, slot]
             picked = picked + ch_in[source, slot].astype(jnp.float32)
         packs.append(total)
@@ -275,12 +314,21 @@
             squares = squares + buf[source, :1]
     out_ref[...] = contrib / jnp.sqrt(squares / tokens + norm_floor)
 
+    def sent_pair(i, carry):
+        for copy in pair_copies(i // own_heads, lax.rem(i, own_heads)):
+            copy.wait_send()
+        return carry
+
+    def sent_owner(to, slot):
+        for copy in owner_copies(to, slot, chip):
+            copy.wait_send()
+
     def sent(peer):
-        for slot in range(own_heads):
-            gram_copy(peer, slot, me).wait_send()
-            ch_copy(peer, slot, me).wait_send()
         solved_copy(peer, me).wait_send()
         norm_copy(seq_norm, seq_sems, "seq", peer, me, me).wait_send()
+
+    lax.fori_loop(0, chips * own_heads, sent_pair, 0)
+    other_chips(sent_owner)
 
     def sent_rep(peer):
         score_copy(peer, layer).wait_send()
@@ -298,8 +346,8 @@
     width, own_heads = cols // heads, heads // n_seq
     queries = query_ids.shape[0]
     out_rows = rows // n_rep
-    pack = (n_seq, own_heads, width // 2 + 8, width + width // 2)
-    picked = (n_seq, own_heads, queries, width)
+    pack = (n_seq // 2, own_heads, width // 2 + 8, width + width // 2)
+    picked = (n_seq // 2, own_heads, queries, width)
     vmem = pl.BlockSpec(memory_space=pltpu.VMEM)
     f32, bf16, dma = jnp.float32, jnp.bfloat16, pltpu.SemaphoreType.DMA
     return pl.pallas_call(
@@ -310,17 +358,14 @@
         scratch_shapes=[
             pltpu.VMEM((rows, cols), bf16),
             pltpu.VMEM((queries, rows), bf16),
-            pltpu.VMEM(pack, f32),
-            pltpu.VMEM(pack, f32),
-            pltpu.VMEM(picked, bf16),
-            pltpu.VMEM(picked, bf16),
+            *[pltpu.VMEM(pack, f32)] * 4,
+            *[pltpu.VMEM(picked, bf16)] * 4,
             pltpu.VMEM((queries, cols), bf16),
             pltpu.VMEM((rows, queries), f32),
             pltpu.VMEM((n_rep, out_rows, queries), f32),
             pltpu.VMEM((n_rep, 8, queries), f32),
             pltpu.VMEM((n_seq, 8, queries), f32),
-            dma((2, n_seq, own_heads)),
-            dma((2, n_seq, own_heads)),
+            *[dma((2, n_seq // 2, own_heads))] * 4,
             dma((2, n_seq)),
             dma((2, n_rep)),
             dma((2, n_rep)),

time: 153 us -> 128 us (0.84)
  Pallas kernels: 149 us -> 124 us
    pallas_call x1, Pallas kernels: 149 us -> 124 us  [on_device(): pl.pallas_call(functools.partial(whole_kernel, math.sqrt(width / depth),...]
where the time goes in v3:
time: 128 us
  Pallas kernels  124 us (97%)
  local copies, waits for them, and re-layouts  3.74 us (3%)
    pallas_call x1, Pallas kernels, on_device(): pl.pallas_call(functools.partial(whole_kernel, math.sqrt(width / depth),...  124 us

profile of v3, /device:TPU:0, one launch (start us, length us, event | category | flops | bytes accessed | tf_op | source)
XLA Modules:
  0.0 127.9 jit_solution(3882100757743694587)
XLA Ops:
  0.0 0.7 convert_element_type.3
  0.7 1.4 %copy.9.ids_ref = s32[64,1]{1,0:T(8,128)} copy(s32[64,1]{0,1:T(1,128)} %bitcast.9) | data formatting | bytes 512 | tf_op jit(solution)/shard_map/broadcast_in_dim | solution.py:383
  2.0 0.8 copy.8.mask_ref
  2.9 123.5 %attribute.1 = f32[128,64]{1,0:T(8,128)} custom-call(bf16[512,3584]{1,0:T(8,128)(2,1)} %bitcast.6, bf16[512,4096]{1,0:T(8,128)(2,1)} %bitcast.5, s32[16,3584]{1,0:T(8,128)} %bitcast.7, f32[512,1]{1,0:T(8,128)} %copy.8.mask_ref, s32[64,1]{1,0:T(8,128)} %copy.9.ids_ref), custom_call_target="tpu_custom_call" | custom-call | tf_op jit(solution)/shard_map/attribute/pallas_call | solution.py:353
  126.4 1.5 %copy.10 = f32[128,64]{0,1:T(8,128)} copy(f32[128,64]{1,0:T(8,128)} %attribute.1) | data formatting | bytes 65536 | tf_op jit(solution)/shard_map/attribute/pallas_call | solution.py:353

commit v4 on v3

--- a/solution.py
+++ b/solution.py
@@ -83,9 +83,10 @@
     grad_ref,
     cols_ref,
     codes_ref,
-    mask_ref,
+    mask_row_ref,
     ids_ref,
     out_ref,
+    mask_ref,
     sk_ref,
     hits_ref,
     gram_stage,
@@ -126,9 +127,10 @@
             ),
         )
 
-    mask = mask_ref[...]
-    count = jnp.sum(mask, axis=0, keepdims=True)
-    token = lax.broadcasted_iota(jnp.int32, (ids_ref.shape[0], rows), 1)
+    mask = mask_row_ref[...].astype(jnp.float32)
+    count = jnp.sum(mask, axis=1, keepdims=True)
+    mask_ref[...] = jnp.transpose(jnp.broadcast_to(mask, (128, rows)))[:, :1]
+    token = lax.broadcasted_iota(jnp.int32, (rows, ids_ref.shape[1]), 0)
     hits_ref[...] = jnp.where(ids_ref[...] - me * rows == token, 1.0, 0.0).astype(jnp.bfloat16)
 
     def sketch_head(head, gram_to, ch_to):
@@ -153,8 +155,8 @@
         gram_to[:half, :width] = gram[:half]
         gram_to[:half, width:] = gram[half:, half:]
         gram_to[half:, :] = jnp.broadcast_to(count, (8, width + half))
-        ch_to[...] = jnp.dot(
-            hits_ref[...], sketch, preferred_element_type=jnp.float32
+        ch_to[...] = lax.dot_general(
+            hits_ref[...], sketch, TN, preferred_element_type=jnp.float32
         ).astype(jnp.bfloat16)
 
     chips = n_seq // 2
@@ -356,8 +358,9 @@
         out_specs=vmem,
         out_shape=jax.ShapeDtypeStruct((out_rows, queries), f32),
         scratch_shapes=[
+            pltpu.VMEM((rows, 1), f32),
             pltpu.VMEM((rows, cols), bf16),
-            pltpu.VMEM((queries, rows), bf16),
+            pltpu.VMEM((rows, queries), bf16),
             *[pltpu.VMEM(pack, f32)] * 4,
             *[pltpu.VMEM(picked, bf16)] * 4,
             pltpu.VMEM((queries, cols), bf16),
@@ -379,8 +382,8 @@
         gradient,
         outputs,
         codes,
-        loss_mask.astype(f32)[:, None],
-        query_ids[:, None],
+        loss_mask[None, :],
+        query_ids[None, :],
     )
 
 

time: 128 us -> 125 us (0.977)
  local copies, waits for them, and re-layouts: 3.74 us -> 1.54 us
    broadcast_in_dim x2 -> x0, local copies, waits for them, and re-layouts: 2.21 us -> none  [the longest x1 1.36 us: on_device(): query_ids[:, None]]
where the time goes in v4:
time: 125 us
  Pallas kernels  123 us (98%)
  local copies, waits for them, and re-layouts  1.54 us (1%)
    pallas_call x1, Pallas kernels, on_device(): pl.pallas_call(functools.partial(whole_kernel, math.sqrt(width / depth),...  123 us

profile of v4, /device:TPU:0, one launch (start us, length us, event | category | flops | bytes accessed | tf_op | source)
XLA Modules:
  0.0 125.0 jit_solution(8297161588795883462)
XLA Ops:
  0.0 123.5 %attribute.1 = f32[128,64]{1,0:T(8,128)} custom-call(bf16[512,3584]{1,0:T(8,128)(2,1)} %bitcast.6, bf16[512,4096]{1,0:T(8,128)(2,1)} %bitcast.5, s32[16,3584]{1,0:T(8,128)} %bitcast.7, s32[1,512]{1,0:T(1,128)} %bitcast.8, s32[1,64]{1,0:T(1,128)} %bitcast.9), custom_call_target="tpu_custom_call" | custom-call | tf_op jit(solution)/shard_map/attribute/pallas_call | solution.py:355
  123.5 1.5 %copy.6 = f32[128,64]{0,1:T(8,128)} copy(f32[128,64]{1,0:T(8,128)} %attribute.1) | data formatting | bytes 65536 | tf_op jit(solution)/shard_map/attribute/pallas_call | solution.py:355
